TPU v7x, 16 devices: a 4x2x1 block of a 4x4x8 slice. The times are simulated.
16 devices in a mesh: dp: 2 (over y, z), tp: 8 (over x, core).
Axes of the slice: x: 4, y: 2, z: 1, core: 2. Of those that a mesh axis runs over, the one named last changes fastest.
The devices are a block of a 4x4x8 slice.
Arguments:
- tokens: bfloat16 [6, 768, 5120], P('dp'), parts along dimension 0
- positions: int32 [6, 768], P('dp'), parts along dimension 0
- lengths: int32 [6], P('dp'), parts along dimension 0
- norm_attn: bfloat16 [5120], replicated
- norm_mlp: bfloat16 [5120], replicated
- q_gain: bfloat16 [128], replicated
- k_gain: bfloat16 [128], replicated
- w_query: bfloat16 [5120, 8192], P(None, 'tp')
- w_key: bfloat16 [5120, 1024], replicated
- w_value: bfloat16 [5120, 1024], replicated
- w_out: bfloat16 [8192, 5120], P('tp')
- w_gate: bfloat16 [5120, 25600], P(None, 'tp')
- w_up: bfloat16 [5120, 25600], P(None, 'tp')
- w_down: bfloat16 [25600, 5120], P('tp')
Outputs:
- output 1: bfloat16 [6, 768, 5120], P('dp'), parts along dimension 0
- output 2: bfloat16 [6, 768, 8, 128], P('dp', None, 'tp'), parts along dimension 0
- output 3: bfloat16 [6, 768, 8, 128], P('dp', None, 'tp'), parts along dimension 0
There are 2 independent parts. A program takes and returns all parts, laid end to end along the dimension named above; an argument that names none is the same for every part.
All inputs are finite; a program needn't handle non-finite values.
Results may differ from a plain program's by a relative error of at most 0.0149066.
Values are sent between devices in bfloat16 or wider.
A program may use at most 768 MiB of HBM per device.

v0:
```python
import functools
import jax
import jax.numpy as jnp
import numpy as np
from jax import lax
from jax.experimental import pallas as pl
from jax.experimental.pallas import tpu as pltpu
from jax.sharding import PartitionSpec as P

EPSILON = 1e-6
ROPE_THETA = 1000000.0
MESH = pl.DeviceIdType.MESH
CORES = 2
TILE = 256
UNITS = 5
HOPS = 6
A_BUFS = 4
X_PARTS = 4
HEADS_AT_ONCE = 4
BF = jnp.bfloat16
F32 = jnp.float32


def dot(a, b):
    return jnp.dot(a, b, preferred_element_type=F32)


def dot_nt(a, b):
    return lax.dot_general(a, b, (((1,), (1,)), ((), ())), preferred_element_type=F32)


def over(x, n):
    return lax.shift_right_logical(x * (65536 // n + 1), 16)


def split(x, n):
    q = over(x, n)
    return q, x - q * n


def pick(i, values):
    out = values[0]
    for n, v in enumerate(values[1:], 1):
        out = jnp.where(i >= n, v, out)
    return out


def layer_kernel(tp, prompts, seq, head_dim, kv_heads, dims,
                 tokens, positions, lens, n_attn, n_mlp, q_gain, k_gain, freq, wq, wk, wv, wo, wg, wu, wdn,
                 ho, kc, vc,
                 n2, act, qs, os, kk, vt, kco, vco, cosb, sinb, ybuf, seen, tri, gains, gu, wd, pp, xp, land, ownh,
                 s_x, s_gu, s_wd, s_stage, s_xp, s_res, s_kv, s_own,
                 rs_send, rs_recv, ag_send, ag_recv, dd_send, dd_recv):
    hidden, width_q, width_f = dims
    chips = tp // CORES
    half = hidden // CORES
    unit = half // UNITS
    rows_b = seq // chips
    heads = width_q // head_dim
    q_tiles = width_q // TILE
    f_tiles = width_f // TILE
    odd = width_f % TILE != 0
    n_tiles = CORES * UNITS
    per_ar = HOPS * UNITS
    lead = UNITS + 1
    last = 2 * prompts - 1
    lanes = head_dim
    add_rows = rows_b // 4 if rows_b % 64 == 0 else 16
    o_bufs = 2 * (width_f // width_q)
    row_groups = min(4, seq // X_PARTS // 16)
    norm_tiles = n_tiles - 2
    norm_rows = seq // norm_tiles
    span_q = min(lanes, seq)
    hidden_score = -1e30 * head_dim ** 0.5
    to_exp2 = head_dim ** -0.5 * 1.4426950408889634

    me = lax.axis_index('tp')
    core = lax.rem(me, CORES)
    chip = me // CORES
    ring = lax.rem(chip + core * (chips - 2 * chip), chips)
    nxt = CORES * lax.rem(chip + chips + 1 - 2 * core, chips) + core
    prv = CORES * lax.rem(chip + chips - 1 + 2 * core, chips) + core
    partner = me + 1 - 2 * core
    kv_col = pl.multiple_of((me // (tp // kv_heads)) * head_dim, head_dim)

    def remote(src, dst, send, recv, to):
        return pltpu.make_async_remote_copy(src_ref=src, dst_ref=dst, send_sem=send, recv_sem=recv,
                                            device_id={'tp': to}, device_id_type=MESH)

    def local(src, dst, sem):
        return pltpu.make_async_copy(src, dst, sem)

    def await_copy(ref, sem):
        local(ref, ref, sem).wait()

    def wrap(b):
        return jnp.where(b < 0, b + chips, b)

    def block_rows(b):
        return pl.ds(pl.multiple_of(b * rows_b, rows_b), rows_b)

    def a_place(t):
        b = t % A_BUFS if isinstance(t, int) else lax.bitwise_and(t, A_BUFS - 1)
        return b, gu.at[b // 2, :, pl.ds(pl.multiple_of(lax.rem(b, 2) * TILE, TILE), TILE)]

    def a_tile(t):
        if isinstance(t, int) and t == 0:
            return (local(wk.at[:, pl.ds(kv_col, lanes)], gu.at[0, :, pl.ds(0, lanes)], s_gu.at[0, 0]),
                    local(wv.at[:, pl.ds(kv_col, lanes)], gu.at[0, :, pl.ds(lanes, lanes)], s_gu.at[0, 1]))
        b, place = a_place(t)
        return (local(wq.at[:, pl.ds(pl.multiple_of((t - 1) * TILE, TILE), TILE)], place, s_gu.at[b, 0]),)

    def f_pair(b, col, width):
        cols = pl.ds(pl.multiple_of(col, lanes), width)
        return (local(wg.at[:, cols], gu.at[b, :, pl.ds(0, width)], s_gu.at[b, 0]),
                local(wu.at[:, cols], gu.at[b, :, pl.ds(width, width)], s_gu.at[b, 1]))

    def f_tile(t):
        return f_pair(lax.rem(t, 2), t * TILE, TILE)

    def f_rest():
        return f_pair(f_tiles % 2, f_tiles * TILE, lanes)

    def start_all(copies):
        for cp in copies:
            cp.start()

    def wait_all(copies):
        for cp in copies:
            cp.wait()

    def out_cols(n):
        side = jnp.where(lax.rem(n, 2) == 0, 1 - core, core)
        return pl.ds(pl.multiple_of(side * half + lax.shift_right_logical(n, 1) * unit, unit), unit)

    def o_place(n):
        b = lax.rem(n, o_bufs)
        return wd.at[b // (o_bufs // 2), pl.ds(pl.multiple_of(lax.rem(b, o_bufs // 2) * width_q, width_q), width_q), :]

    def o_tile(n):
        return local(wo.at[:, out_cols(n)], o_place(n), s_wd.at[lax.rem(n, o_bufs)])

    def d_place(n):
        return wd.at[lax.rem(n, 2)]

    def d_tile(n):
        return local(wdn.at[:, out_cols(n)], d_place(n), s_wd.at[lax.rem(n, 2)])

    def load_rows(src, i):
        part = seq // X_PARTS
        return [local(src.at[pl.ds(pl.multiple_of(i * seq + b * part, part), part), :], n2.at[pl.ds(b * part, part), :], s_x.at[b])
                for b in range(X_PARTS)]

    start_all(load_rows(tokens, 0))
    for t in range(A_BUFS - 1):
        start_all(a_tile(t))
    for n in range(o_bufs - 1):
        o_tile(n).start()
    for i in range(prompts):
        for g in range(UNITS):
            rows = pl.ds(pl.multiple_of(i * seq + ring * rows_b, rows_b), rows_b)
            cols = pl.ds(pl.multiple_of(core * half + g * unit, unit), unit)
            local(tokens.at[rows, cols], ownh.at[i * UNITS + g], s_res.at[i * UNITS + g]).start()
    barrier = pltpu.get_barrier_semaphore()
    for other in (nxt, prv, partner):
        pl.semaphore_signal(barrier, inc=1, device_id={'tp': other}, device_id_type=MESH)

    for v, gain in enumerate((n_attn, n_mlp)):
        wide = gain[...].astype(F32)
        for j in range(hidden // lanes):
            gains[v, :, j * lanes:(j + 1) * lanes] = jnp.broadcast_to(wide[None, j * lanes:(j + 1) * lanes], (16, lanes))
    key_at = lax.broadcasted_iota(jnp.int32, (span_q, span_q), 0)
    tri[...] = jnp.where(key_at <= lax.broadcasted_iota(jnp.int32, (span_q, span_q), 1), 1.0, 0.0)
    pl.semaphore_wait(barrier, 3)

    def ho_block(c, g, b, side):
        rows = pl.ds(pl.multiple_of(c * seq + b * rows_b, rows_b), rows_b)
        return ho.at[rows, pl.ds(pl.multiple_of(side * half + g * unit, unit), unit)]

    def send_partial(e, c, g):
        par = lax.bitwise_and(c, 1)
        u = par * UNITS + g
        rows = block_rows(wrap(ring - 1 - e))
        with jax.named_scope('w_rs'):
            if e == 0:
                await_copy(xp.at[u], s_xp.at[u])
            else:
                await_copy(land.at[par, g, e - 1], rs_recv.at[par, g, e - 1])
        mine, theirs, came = pp.at[u, rows], xp.at[u, rows], land.at[par, g, max(e - 1, 0)]

        def add(r, _):
            rr = pl.ds(pl.multiple_of(r * add_rows, 16), add_rows)
            total = mine[rr, :].astype(F32) + theirs[rr, :].astype(F32)
            if e > 0:
                total = total + came[rr, :].astype(F32)
            mine[rr, :] = total.astype(BF)
            return 0
        lax.fori_loop(0, rows_b // add_rows, add, 0)
        remote(mine, land.at[par, g, e], rs_send.at[par, g, e], rs_recv.at[par, g, e], nxt).start()

    def finish_sum(c, g):
        par = lax.bitwise_and(c, 1)
        u, w = par * UNITS + g, jnp.where(c < prompts, c, c - prompts) * UNITS + g
        rows = block_rows(ring)
        with jax.named_scope('w_rs3'):
            await_copy(land.at[par, g, 2], rs_recv.at[par, g, 2])

        @pl.when(c < prompts)
        def _():
            await_copy(ownh.at[w], s_res.at[w])
        mine, theirs, came, own = pp.at[u, rows], xp.at[u, rows], land.at[par, g, 2], ownh.at[w]

        def add(r, _):
            rr = pl.ds(pl.multiple_of(r * add_rows, 16), add_rows)
            total = came[rr, :].astype(F32) + (mine[rr, :].astype(F32) + theirs[rr, :].astype(F32))
            own[rr, :] = (own[rr, :].astype(F32) + total).astype(BF)
            return 0
        lax.fori_loop(0, rows_b // add_rows, add, 0)
        place = ho_block(c, g, ring, core)
        remote(own, place, ag_send.at[par, g, 0], ag_recv.at[par, g, 0], nxt).start()
        remote(own, place, dd_send.at[par, g, 0], dd_recv.at[par, g, 0], partner).start()
        local(own, place, s_own.at[par, g]).start()

    def pass_on(e, c, g):
        par = lax.bitwise_and(c, 1)
        place = ho_block(c, g, wrap(ring - e), core)
        with jax.named_scope('w_ag'):
            await_copy(place, ag_recv.at[par, g, e - 1])
        if e < 3:
            remote(place, place, ag_send.at[par, g, e], ag_recv.at[par, g, e], nxt).start()
        remote(place, place, dd_send.at[par, g, e], dd_recv.at[par, g, e], partner).start()
        if e == 1:
            await_copy(place, dd_recv.at[par, g, 0])
            for s in range(3):
                await_copy(land.at[par, g, s], rs_send.at[par, g, s])

    def settle(c, g):
        par = lax.bitwise_and(c, 1)
        place = ho_block(c, g, ring, core)
        await_copy(land.at[par, g, 0], s_own.at[par, g])
        for e in range(3):
            await_copy(place, ag_send.at[par, g, e])
        for e in range(4):
            await_copy(place, dd_send.at[par, g, e])
        for e in range(1, 4):
            await_copy(place, dd_recv.at[par, g, e])

    def slot(k):
        c = jnp.minimum(over(k, per_ar), last)
        diagonal = c == last
        d, q = split(k - c * per_ar, UNITS)
        g_d = jnp.minimum(d, UNITS - 1) - q
        e_d = jnp.where(g_d >= 0, d - g_d, HOPS)
        e = jnp.where(diagonal, e_d, d)
        g = jnp.where(diagonal, jnp.maximum(g_d, 0), q)
        @pl.when(e < 3)
        def _():
            for s in range(3):
                @pl.when(e == s)
                def _(s=s):
                    send_partial(s, c, g)
                    if s == 0:
                        @pl.when(c > 0)
                        def _():
                            pass_on(3, c - 1, g)

                            @pl.when((g > 0) & jnp.logical_not(diagonal))
                            def _():
                                settle(c - 1, g - 1)
                    if s == 1:
                        @pl.when((c > 0) & (diagonal | (g == 0)))
                        def _():
                            settle(c - 1, jnp.where(diagonal, g, UNITS - 1))

        @pl.when(e >= 3)
        def _():
            @pl.when(e == 3)
            def _():
                finish_sum(c, g)
            for s in range(2):
                @pl.when(e == 4 + s)
                def _(s=s):
                    pass_on(s + 1, c, g)

    def run_slots(lo, hi):
        def body(k, _):
            slot(k)
            return 0
        lax.fori_loop(lo, hi, body, 0)

    def norm_all(v):
        part = seq // X_PARTS
        for b in range(X_PARTS):
            await_copy(n2.at[pl.ds(b * part, part), :], s_x.at[b])

            def scales(r, _):
                for q in range(row_groups):
                    rr = pl.ds(pl.multiple_of(b * part + (r * row_groups + q) * 16, 16), 16)
                    acc = jnp.zeros((16, lanes), F32)
                    for j in range(hidden // lanes):
                        x = n2[rr, j * lanes:(j + 1) * lanes].astype(F32)
                        acc = acc + x * x
                    scale = lax.rsqrt(jnp.sum(acc, axis=-1, keepdims=True) * (1.0 / hidden) + EPSILON)
                    ybuf[0, rr, :lanes] = jnp.broadcast_to(scale, (16, lanes))
                return 0
            lax.fori_loop(0, part // 16 // row_groups, scales, 0)

        def apply(r, _):
            rr = pl.ds(pl.multiple_of(r * 16, 16), 16)
            scale = ybuf[0, rr, :lanes]
            for j in range(hidden // lanes):
                cols = slice(j * lanes, (j + 1) * lanes)
                n2[rr, cols] = (n2[rr, cols].astype(F32) * scale * gains[v, :, cols]).astype(BF)
            return 0
        lax.fori_loop(0, seq // 16, apply, 0)

    def norm_some(v, first):
        for q in range(norm_rows // 16):
            rr = pl.ds(pl.multiple_of(first + q * 16, 16), 16)
            acc = jnp.zeros((16, lanes), F32)
            for j in range(hidden // lanes):
                x = n2[rr, j * lanes:(j + 1) * lanes].astype(F32)
                acc = acc + x * x
            scale = jnp.broadcast_to(lax.rsqrt(jnp.sum(acc, axis=-1, keepdims=True) * (1.0 / hidden) + EPSILON), (16, lanes))
            for j in range(hidden // lanes):
                cols = slice(j * lanes, (j + 1) * lanes)
                n2[rr, cols] = (n2[rr, cols].astype(F32) * scale * gains[v, :, cols]).astype(BF)

    def project(lhs, fetch, place, ahead, c, v, bounds, begin, loaded):
        par = lax.bitwise_and(c, 1)

        def tile(n, norm):
            @pl.when(n + ahead < n_tiles)
            def _():
                fetch(n + ahead).start()
            with jax.named_scope('w_wd'):
                fetch(n).wait()
            g = n // 2
            away = lax.rem(n, 2) == 0
            count = c * UNITS + g
            stage = lax.rem(count, 2)
            u = jnp.where(away, 2 * UNITS + stage, par * UNITS + g)

            @pl.when(away & (count >= 2))
            def _():
                await_copy(pp.at[u], s_stage.at[stage])
            if norm:
                norm_some(v, pl.multiple_of((n - 2) * norm_rows, 16))
            pp[u] = dot(lhs[...], place(n)[...]).astype(BF)

            @pl.when(away)
            def _():
                to = par * UNITS + g
                remote(pp.at[u], xp.at[to], s_stage.at[stage], s_xp.at[to], partner).start()
            run_slots(*bounds(n))

        def plain(n, _):
            tile(n, False)
            return 0

        def normed(n, _):
            tile(n, True)
            return 0
        lax.fori_loop(0, 1, plain, 0)
        begin()
        lax.fori_loop(1, 2, plain, 0)
        loaded()
        lax.fori_loop(2, n_tiles, normed, 0)

    def turned(v, gain):
        v = v * lax.rsqrt(jnp.mean(v * v, axis=-1, keepdims=True) + EPSILON) * gain[...].astype(F32)[None]
        return v * cosb[...] + pltpu.roll(v, lanes // 2, 1) * sinb[...]

    def rope_rows(i):
        where = jnp.broadcast_to(positions[pl.ds(i, 1), :].astype(F32), (lanes, seq)).T * freq[...]
        sine = jnp.sin(where)
        cosb[...] = jnp.cos(where)
        sinb[...] = jnp.where(lax.broadcasted_iota(jnp.int32, (seq, lanes), 1) < lanes // 2, -sine, sine)

    def keep_kv(y, length):
        k_rot = turned(y[:, :lanes], k_gain)
        v_val = y[:, lanes:]
        kk[...] = k_rot.astype(BF)
        vt[...] = v_val.T.astype(BF)
        valid = lax.broadcasted_iota(jnp.int32, (seq, lanes), 0) < length
        seen[...] = jnp.where(valid, 1.0, 0.0)
        kco[...] = jnp.where(valid, k_rot, 0.0).astype(BF)
        vco[...] = jnp.where(valid, v_val, 0.0).astype(BF)

    def keep_q(t, y):
        for s in range(TILE // lanes):
            qs[:, pl.ds(pl.multiple_of(t * TILE + s * lanes, lanes), lanes)] = turned(y[:, s * lanes:(s + 1) * lanes], q_gain).astype(BF)

    def attend(hd):
        cols = pl.ds(pl.multiple_of(hd * lanes, lanes), lanes)
        for lo in range(0, seq, span_q):
            hi = lo + span_q
            q = qs[lo:hi, cols]
            s = dot_nt(kk[:hi, :], q)
            parts = [jnp.where((seen[lo:hi, :span_q] > 0.0) & (tri[...] > 0.0), s[lo:hi, :], hidden_score)]
            for r in range(0, lo, span_q):
                parts.append(jnp.where(seen[r:r + span_q, :span_q] > 0.0, s[r:r + span_q, :], hidden_score))
            top = parts[0].max(0, keepdims=True)
            for x in parts[1:]:
                top = jnp.maximum(top, x.max(0, keepdims=True))
            parts = [jnp.exp2((x - top) * to_exp2) for x in parts]
            total = parts[0].sum(0, keepdims=True)
            for x in parts[1:]:
                total = total + x.sum(0, keepdims=True)
            scale = 1.0 / total
            probs = [(x * scale).astype(BF) for x in parts[1:] + parts[:1]]
            probs = jnp.concatenate(probs, axis=0) if len(probs) > 1 else probs[0]
            os[lo:hi, cols] = dot(vt[:, :hi], probs).T.astype(BF)

    step_a = (per_ar + lead - UNITS) // (prompts - 1)
    w_q, w_h, w_o = 4, 7, 2
    weight_a = w_q * (q_tiles + 1) + w_h * (heads // HEADS_AT_ONCE) + w_o * n_tiles

    with jax.named_scope('norm_x'):
        norm_all(0)

    def attention_phase(i, _):
        def upto(w):
            return jnp.where(i == 0, 0, UNITS + (i - 1) * step_a + over(w * step_a, weight_a))
        length = lens[i]
        def kv_body(t, _):
            start_all(a_tile(A_BUFS - 1))
            with jax.named_scope('qkv'):
                wait_all(a_tile(0))
                rope_rows(i)
                ybuf[0] = dot(n2[...], a_place(0)[1][...])
            return 0
        lax.fori_loop(i, i + 1, kv_body, 0)

        def q0_body(t, _):
            start_all(a_tile(A_BUFS))
            with jax.named_scope('qkv'):
                wait_all(a_tile(1))
                keep_kv(ybuf[0], length)
                ybuf[1] = dot(n2[...], a_place(1)[1][...])
            return 0
        lax.fori_loop(i, i + 1, q0_body, 0)
        run_slots(upto(0), upto(2 * w_q))

        def q_body(t, _):
            with jax.named_scope('qkv'):
                wait_all(a_tile(t))
                keep_q(t - 2, ybuf[lax.rem(t - 1, 2)])
                ybuf[lax.rem(t, 2)] = dot(n2[...], a_place(t)[1][...])
            run_slots(upto(t * w_q), upto((t + 1) * w_q))
            return 0
        lax.fori_loop(2, q_tiles + 1, q_body, 0)

        @pl.when(i + 1 < prompts)
        def _():
            start_all(load_rows(tokens, i + 1))
            for t in range(A_BUFS - 1):
                start_all(a_tile(t))

        @pl.when(i + 1 == prompts)
        def _():
            start_all(f_tile(0))
        rows = pl.ds(pl.multiple_of(i * seq, seq), seq)
        caches = (local(kco, kc.at[rows, :], s_kv.at[0]), local(vco, vc.at[rows, :], s_kv.at[1]))
        start_all(caches)
        with jax.named_scope('keep_q'):
            keep_q(q_tiles - 1, ybuf[q_tiles % 2])
        base1 = (q_tiles + 1) * w_q

        def heads_body(t, _):
            with jax.named_scope('attend'):
                for hd in range(HEADS_AT_ONCE):
                    attend(t * HEADS_AT_ONCE + hd)
            run_slots(upto(base1 + t * w_h), upto(base1 + (t + 1) * w_h))
            return 0
        lax.fori_loop(0, heads // HEADS_AT_ONCE, heads_body, 0)
        base = base1 + heads // HEADS_AT_ONCE * w_h
        wait_all(caches)

        def bounds(n):
            return (jnp.where(i == 0, n // 2, upto(base + n * w_o)),
                    jnp.where(i == 0, (n + 1) // 2, upto(base + (n + 1) * w_o)))

        def loaded():
            @pl.when(i + 1 < prompts)
            def _():
                wait_all(load_rows(tokens, i + 1))
        with jax.named_scope('project_o'):
            project(os, o_tile, o_place, o_bufs - 1, i, 0, bounds, lambda: None, loaded)

        @pl.when(i + 1 < prompts)
        def _():
            for n in range(o_bufs - 1):
                o_tile(n).start()

        @pl.when(i + 1 == prompts)
        def _():
            d_tile(0).start()
        return 0
    lax.fori_loop(0, prompts, attention_phase, 0)

    a_end = UNITS + (prompts - 1) * step_a
    with jax.named_scope('pre_mlp'):
        run_slots(a_end, per_ar + lead)
    start_all(load_rows(ho, 0))
    with jax.named_scope('norm_h'):
        norm_all(1)
    starts = [(m + 1) * per_ar + v for m, v in zip(range(prompts), (lead, 18, 32))]
    mids = [(m + 2) * per_ar + v for m, v in zip(range(prompts), (3, 15, 30))]
    ones = [max((m + 2) * per_ar + lead, mids[m] + 2) if m + 1 < prompts else mids[m] for m in range(prompts)]
    ends = starts[1:] + [last * per_ar + UNITS * UNITS]

    soon = [0, 0, 1]
    for g in range(1, UNITS):
        soon += [g * UNITS, g * UNITS + (g + 2) // 2]
    soon = soon[:n_tiles] + [UNITS * UNITS]

    def mlp_phase(i, _):
        k0, k1, kt, k2 = pick(i, starts), pick(i, mids), pick(i, ones), pick(i, ends)

        def gated(y, width):
            gate, up = y[:, :width], y[:, width:]
            return (gate * jax.nn.sigmoid(gate) * up).astype(BF)

        def f_body(t, _):
            @pl.when(t + 1 < f_tiles)
            def _():
                start_all(f_tile(t + 1))
            if odd:
                @pl.when(t + 1 == f_tiles)
                def _():
                    start_all(f_rest())
            with jax.named_scope('w_gu'):
                wait_all(f_tile(t))
            act[:, pl.ds(pl.multiple_of(t * TILE, TILE), TILE)] = gated(dot(n2[...], gu[lax.rem(t, 2)]), TILE)
            run_slots(k0 + over(t * (k1 - k0), f_tiles), k0 + over((t + 1) * (k1 - k0), f_tiles))
            return 0
        with jax.named_scope('f_loop'):
            lax.fori_loop(0, f_tiles, f_body, 0)
        if odd:
            def rest_body(t, _):
                with jax.named_scope('f_rest'):
                    wait_all(f_rest())
                    act[:, f_tiles * TILE:] = gated(dot(n2[...], gu[f_tiles % 2, :, :TILE]), lanes)
                return 0
            lax.fori_loop(i, i + 1, rest_body, 0)

        @pl.when(i + 1 < prompts)
        def _():
            start_all(f_tile(0))

        def upto(n):
            spread = jnp.where(n <= 1, k1 + n * (kt - k1), kt + over(jnp.maximum(n - 1, 0) * (k2 - kt), n_tiles - 1))
            return jnp.where(i == prompts - 1, k1 + pick(n, soon), spread)

        def begin():
            @pl.when(i + 1 < prompts)
            def _():
                start_all(load_rows(ho, i + 1))

        def loaded():
            @pl.when(i + 1 < prompts)
            def _():
                wait_all(load_rows(ho, i + 1))
        with jax.named_scope('project_d'):
            project(act, d_tile, d_place, 1, prompts + i, 1, lambda n: (upto(n), upto(n + 1)), begin, loaded)

        @pl.when(i + 1 < prompts)
        def _():
            d_tile(0).start()
        return 0
    lax.fori_loop(0, prompts, mlp_phase, 0)

    with jax.named_scope('tail'):
        run_slots(last * per_ar + UNITS * UNITS, last * per_ar + (UNITS + HOPS - 1) * UNITS)

        def ring_end(g, _):
            pass_on(3, last, g)
            return 0
        lax.fori_loop(0, UNITS, ring_end, 0)

        def all_end(g, _):
            settle(last, g)
            return 0
        lax.fori_loop(0, UNITS, all_end, 0)
        for s in range(2):
            await_copy(pp.at[2 * UNITS + s], s_stage.at[s])


def copy_kernel(a, b, c, a_out, b_out, c_out):
    a_out[...] = a[...]
    b_out[...] = b[...]
    c_out[...] = c[...]


def layer_body(tokens, positions, lengths, norm_attn, norm_mlp, q_gain, k_gain, w_query, w_key, w_value, w_out, w_gate, w_up, w_down, tp_size):
    prompts, seq, hidden = tokens.shape
    head_dim = q_gain.shape[0]
    width_q, width_f = w_query.shape[1], w_gate.shape[1]
    kv_heads = w_key.shape[1] // head_dim
    chips = tp_size // CORES
    unit = hidden // CORES // UNITS
    rows_n = prompts * seq
    inv_freq = ROPE_THETA ** (-np.arange(head_dim // 2) / (head_dim // 2))
    freq = jnp.asarray(np.concatenate([inv_freq, inv_freq])[None], F32)
    any_spec = pl.BlockSpec(memory_space=pl.ANY)
    vmem = pl.BlockSpec(memory_space=pltpu.VMEM)
    smem = pl.BlockSpec(memory_space=pltpu.SMEM)
    kernel = functools.partial(layer_kernel, tp_size, prompts, seq, head_dim, kv_heads, (hidden, width_q, width_f))
    dma = pltpu.SemaphoreType.DMA
    o_bufs = 2 * (width_f // width_q)
    span_q = min(head_dim, seq)
    ho, kc, vc = pl.pallas_call(
        kernel,
        name='decoder_layer',
        out_shape=(jax.ShapeDtypeStruct((2 * rows_n, hidden), BF),
                   jax.ShapeDtypeStruct((rows_n, head_dim), BF),
                   jax.ShapeDtypeStruct((rows_n, head_dim), BF)),
        in_specs=[any_spec, vmem, smem, vmem, vmem, vmem, vmem, vmem] + [any_spec] * 7,
        out_specs=(any_spec, any_spec, any_spec),
        scratch_shapes=[
            pltpu.VMEM((seq, hidden), BF),
            pltpu.VMEM((seq, width_f), BF),
            pltpu.VMEM((seq, width_q), BF), pltpu.VMEM((seq, width_q), BF),
            pltpu.VMEM((seq, head_dim), BF), pltpu.VMEM((head_dim, seq), BF),
            pltpu.VMEM((seq, head_dim), BF), pltpu.VMEM((seq, head_dim), BF),
            pltpu.VMEM((seq, head_dim), F32), pltpu.VMEM((seq, head_dim), F32),
            pltpu.VMEM((2, seq, TILE), F32),
            pltpu.VMEM((seq, head_dim), F32),
            pltpu.VMEM((span_q, span_q), F32),
            pltpu.VMEM((2, 16, hidden), F32),
            pltpu.VMEM((2, hidden, 2 * TILE), BF),
            pltpu.VMEM((2, width_f, unit), BF),
            pltpu.VMEM((2 * UNITS + 2, seq, unit), BF),
            pltpu.VMEM((2 * UNITS, seq, unit), BF),
            pltpu.VMEM((2, UNITS, 3, seq // chips, unit), BF),
            pltpu.VMEM((prompts * UNITS, seq // chips, unit), BF),
            dma((X_PARTS,)), dma((A_BUFS, 2)), dma((o_bufs,)), dma((2,)), dma((2 * UNITS,)), dma((prompts * UNITS,)), dma((2,)), dma((2, UNITS)),
            dma((2, UNITS, 3)), dma((2, UNITS, 3)), dma((2, UNITS, 3)), dma((2, UNITS, 3)), dma((2, UNITS, 4)), dma((2, UNITS, 4)),
        ],
        compiler_params=pltpu.CompilerParams(collective_id=0, has_side_effects=True, vmem_limit_bytes=67043328),
    )(tokens.reshape(rows_n, hidden), positions, lengths, norm_attn, norm_mlp, q_gain, k_gain, freq,
      w_query, w_key, w_value, w_out, w_gate, w_up, w_down)
    shape = (prompts, seq, 1, head_dim)
    parts = 2 * prompts
    block = rows_n // parts
    out, kc, vc = pl.pallas_call(
        copy_kernel,
        name='copy_out',
        grid=(parts,),
        out_shape=(jax.ShapeDtypeStruct((rows_n, hidden), BF), jax.ShapeDtypeStruct(kc.shape, BF), jax.ShapeDtypeStruct(vc.shape, BF)),
        in_specs=[pl.BlockSpec((block, hidden), lambda b: (b + parts, 0))] + [pl.BlockSpec((block, head_dim), lambda b: (b, 0))] * 2,
        out_specs=[pl.BlockSpec((block, hidden), lambda b: (b, 0))] + [pl.BlockSpec((block, head_dim), lambda b: (b, 0))] * 2,
        compiler_params=pltpu.CompilerParams(vmem_limit_bytes=40 * 1024 * 1024),
    )(ho, kc, vc)
    return out.reshape(prompts, seq, hidden), kc.reshape(shape), vc.reshape(shape)


def solution(mesh):
    body = functools.partial(layer_body, tp_size=mesh.shape['tp'])
    in_specs = (P('dp', None, None), P('dp', None), P('dp'), P(), P(), P(), P(), P(None, 'tp'), P(), P(), P('tp', None), P(None, 'tp'), P(None, 'tp'), P('tp', None))
    out_specs = (P('dp', None, None), P('dp', None, 'tp', None), P('dp', None, 'tp', None))
    return jax.shard_map(body, mesh=mesh, in_specs=in_specs, out_specs=out_specs, check_vma=False)
```

profile of v0, /device:TPU:113, one launch (start us, length us, event | category | flops | bytes accessed | tf_op | source)
XLA Modules:
  0.0 476.9 jit_solution(6455671541890212621)
XLA Ops:
  0.6 457.8 %decoder_layer.1 = (bf16[4608,5120]{1,0:T(8,128)(2,1)}, bf16[2304,128]{1,0:T(8,128)(2,1)}, bf16[2304,128]{1,0:T(8,128)(2,1)}) custom-call(bf16[2304,5120]{1,0:T(8,128)(2,1)} %bitcast.8, s32[3,768]{1,0:T(4,128)} %positions.1, s32[3]{0:T(128)} %lens.1, bf16[5120]{0:T(1024)(128)(2,1)} %n_attn.1, bf16[5120]{0:T(1024)(128)(2,1)} %n_mlp.1, bf16[128]{0:T(256)(128)(2,1)} %q_gain.1, ...), custom_call_target="tpu_custom_call" | custom-call | tf_op jit(solution)/shard_map/decoder_layer/pallas_call | solution.py:613
  458.4 0.0 copy-start
  458.4 1.1 copy-done
  459.5 0.0 copy-start.1
  459.5 1.1 copy-done.1
  460.5 16.4 %copy_out.1 = (bf16[2304,5120]{1,0:T(8,128)(2,1)}, bf16[2304,128]{1,0:T(8,128)(2,1)}, bf16[2304,128]{1,0:T(8,128)(2,1)}) custom-call(bf16[4608,5120]{1,0:T(8,128)(2,1)} %get-tuple-element.9.a, bf16[2304,128]{1,0:T(8,128)(2,1)S(1)} %copy-done, bf16[2304,128]{1,0:T(8,128)(2,1)S(1)} %copy-done.1), custom_call_target="tpu_custom_call" | custom-call | tf_op jit(solution)/shard_map/copy_out/pallas_call | solution.py:647
Async XLA Ops:
  458.4 1.1 copy-start
  459.5 1.1 copy-start.1
where the time goes:
time: 477 us
  Pallas kernels  474 us (99%)
    pallas_call x1, Pallas kernels, layer_body(): pl.pallas_call(kernel, name='decoder_layer', out_shape=(jax.ShapeDtypeStr...  458 us
    pallas_call x1, Pallas kernels, layer_body(): pl.pallas_call(copy_kernel, name='copy_out', grid=(parts,), out_shape=(ja...  16.4 us

commit v1 on v0

--- a/solution.py
+++ b/solution.py
@@ -67,7 +67,7 @@
     lanes = head_dim
     add_rows = rows_b // 4 if rows_b % 64 == 0 else 16
     o_bufs = 2 * (width_f // width_q)
-    row_groups = min(4, seq // X_PARTS // 16)
+    row_groups = min(6, seq // X_PARTS // 16)
     norm_tiles = n_tiles - 2
     norm_rows = seq // norm_tiles
     span_q = min(lanes, seq)
@@ -154,13 +154,6 @@
     start_all(load_rows(tokens, 0))
     for t in range(A_BUFS - 1):
         start_all(a_tile(t))
-    for n in range(o_bufs - 1):
-        o_tile(n).start()
-    for i in range(prompts):
-        for g in range(UNITS):
-            rows = pl.ds(pl.multiple_of(i * seq + ring * rows_b, rows_b), rows_b)
-            cols = pl.ds(pl.multiple_of(core * half + g * unit, unit), unit)
-            local(tokens.at[rows, cols], ownh.at[i * UNITS + g], s_res.at[i * UNITS + g]).start()
     barrier = pltpu.get_barrier_semaphore()
     for other in (nxt, prv, partner):
         pl.semaphore_signal(barrier, inc=1, device_id={'tp': other}, device_id_type=MESH)
@@ -418,6 +411,13 @@
 
     with jax.named_scope('norm_x'):
         norm_all(0)
+    for n in range(o_bufs - 1):
+        o_tile(n).start()
+    for i in range(prompts):
+        for g in range(UNITS):
+            rows = pl.ds(pl.multiple_of(i * seq + ring * rows_b, rows_b), rows_b)
+            cols = pl.ds(pl.multiple_of(core * half + g * unit, unit), unit)
+            local(tokens.at[rows, cols], ownh.at[i * UNITS + g], s_res.at[i * UNITS + g]).start()
 
     def attention_phase(i, _):
         def upto(w):
@@ -642,7 +642,7 @@
     )(tokens.reshape(rows_n, hidden), positions, lengths, norm_attn, norm_mlp, q_gain, k_gain, freq,
       w_query, w_key, w_value, w_out, w_gate, w_up, w_down)
     shape = (prompts, seq, 1, head_dim)
-    parts = 2 * prompts
+    parts = 4 * prompts
     block = rows_n // parts
     out, kc, vc = pl.pallas_call(
         copy_kernel,
@@ -651,7 +651,7 @@
         out_shape=(jax.ShapeDtypeStruct((rows_n, hidden), BF), jax.ShapeDtypeStruct(kc.shape, BF), jax.ShapeDtypeStruct(vc.shape, BF)),
         in_specs=[pl.BlockSpec((block, hidden), lambda b: (b + parts, 0))] + [pl.BlockSpec((block, head_dim), lambda b: (b, 0))] * 2,
         out_specs=[pl.BlockSpec((block, hidden), lambda b: (b, 0))] + [pl.BlockSpec((block, head_dim), lambda b: (b, 0))] * 2,
-        compiler_params=pltpu.CompilerParams(vmem_limit_bytes=40 * 1024 * 1024),
+        compiler_params=pltpu.CompilerParams(vmem_limit_bytes=60 * 1024 * 1024),
     )(ho, kc, vc)
     return out.reshape(prompts, seq, hidden), kc.reshape(shape), vc.reshape(shape)
 

time: 477 us -> 480 us (level)
  Pallas kernels: 474 us -> 479 us
where the time goes in v1:
time: 480 us; the launch traced here: 479 us
  Pallas kernels  479 us (100%)
    pallas_call x1, Pallas kernels, layer_body(): pl.pallas_call(kernel, name='decoder_layer', out_shape=(jax.ShapeDtypeStr...  458 us
    pallas_call x1, Pallas kernels, layer_body(): pl.pallas_call(copy_kernel, name='copy_out', grid=(parts,), out_shape=(ja...  20.2 us

profile of v1, /device:TPU:113, one launch (start us, length us, event | category | flops | bytes accessed | tf_op | source)
XLA Modules:
  0.0 479.4 jit_solution(11621631734895086895)
XLA Ops:
  0.6 458.5 %decoder_layer.1 = (bf16[4608,5120]{1,0:T(8,128)(2,1)}, bf16[2304,128]{1,0:T(8,128)(2,1)}, bf16[2304,128]{1,0:T(8,128)(2,1)}) custom-call(bf16[2304,5120]{1,0:T(8,128)(2,1)} %bitcast.8, s32[3,768]{1,0:T(4,128)} %positions.1, s32[3]{0:T(128)} %lens.1, bf16[5120]{0:T(1024)(128)(2,1)} %n_attn.1, bf16[5120]{0:T(1024)(128)(2,1)} %n_mlp.1, bf16[128]{0:T(256)(128)(2,1)} %q_gain.1, ...), custom_call_target="tpu_custom_call" | custom-call | tf_op jit(solution)/shard_map/decoder_layer/pallas_call | solution.py:613
  459.1 20.2 %copy_out.1 = (bf16[2304,5120]{1,0:T(8,128)(2,1)}, bf16[2304,128]{1,0:T(8,128)(2,1)}, bf16[2304,128]{1,0:T(8,128)(2,1)}) custom-call(bf16[4608,5120]{1,0:T(8,128)(2,1)} %get-tuple-element.9.a, bf16[2304,128]{1,0:T(8,128)(2,1)} %get-tuple-element.10.b, bf16[2304,128]{1,0:T(8,128)(2,1)} %get-tuple-element.11.c), custom_call_target="tpu_custom_call" | custom-call | tf_op jit(solution)/shard_map/copy_out/pallas_call | solution.py:647

commit v2 on v1

--- a/solution.py
+++ b/solution.py
@@ -164,7 +164,6 @@
             gains[v, :, j * lanes:(j + 1) * lanes] = jnp.broadcast_to(wide[None, j * lanes:(j + 1) * lanes], (16, lanes))
     key_at = lax.broadcasted_iota(jnp.int32, (span_q, span_q), 0)
     tri[...] = jnp.where(key_at <= lax.broadcasted_iota(jnp.int32, (span_q, span_q), 1), 1.0, 0.0)
-    pl.semaphore_wait(barrier, 3)
 
     def ho_block(c, g, b, side):
         rows = pl.ds(pl.multiple_of(c * seq + b * rows_b, rows_b), rows_b)
@@ -405,12 +404,13 @@
             probs = jnp.concatenate(probs, axis=0) if len(probs) > 1 else probs[0]
             os[lo:hi, cols] = dot(vt[:, :hi], probs).T.astype(BF)
 
-    step_a = (per_ar + lead - UNITS) // (prompts - 1)
+    step_a = (per_ar + lead - UNITS + 1) // (prompts - 1)
     w_q, w_h, w_o = 4, 7, 2
     weight_a = w_q * (q_tiles + 1) + w_h * (heads // HEADS_AT_ONCE) + w_o * n_tiles
 
     with jax.named_scope('norm_x'):
         norm_all(0)
+    pl.semaphore_wait(barrier, 3)
     for n in range(o_bufs - 1):
         o_tile(n).start()
     for i in range(prompts):
@@ -421,7 +421,7 @@
 
     def attention_phase(i, _):
         def upto(w):
-            return jnp.where(i == 0, 0, UNITS + (i - 1) * step_a + over(w * step_a, weight_a))
+            return jnp.where(i == 0, 0, UNITS - 1 + (i - 1) * step_a + over(w * step_a, weight_a))
         length = lens[i]
         def kv_body(t, _):
             start_all(a_tile(A_BUFS - 1))
@@ -478,8 +478,9 @@
         wait_all(caches)
 
         def bounds(n):
-            return (jnp.where(i == 0, n // 2, upto(base + n * w_o)),
-                    jnp.where(i == 0, (n + 1) // 2, upto(base + (n + 1) * w_o)))
+            early = lax.shift_right_logical(jnp.maximum(n - 2, 0), 1), lax.shift_right_logical(jnp.maximum(n - 1, 0), 1)
+            return (jnp.where(i == 0, early[0], upto(base + n * w_o)),
+                    jnp.where(i == 0, early[1], upto(base + (n + 1) * w_o)))
 
         def loaded():
             @pl.when(i + 1 < prompts)
@@ -499,7 +500,7 @@
         return 0
     lax.fori_loop(0, prompts, attention_phase, 0)
 
-    a_end = UNITS + (prompts - 1) * step_a
+    a_end = UNITS - 1 + (prompts - 1) * step_a
     with jax.named_scope('pre_mlp'):
         run_slots(a_end, per_ar + lead)
     start_all(load_rows(ho, 0))
@@ -587,10 +588,17 @@
             await_copy(pp.at[2 * UNITS + s], s_stage.at[s])
 
 
-def copy_kernel(a, b, c, a_out, b_out, c_out):
-    a_out[...] = a[...]
-    b_out[...] = b[...]
-    c_out[...] = c[...]
+def copy_kernel(first, a, b, c, a_out, b_out, c_out, a_buf, b_buf, c_buf, s_in, s_out):
+    pieces, rows = a_buf.shape[0], a_buf.shape[1]
+    moves = [(a.at[pl.ds(first + p * rows, rows), :], a_buf.at[p], a_out.at[pl.ds(p * rows, rows), :]) for p in range(pieces)]
+    moves += [(b, b_buf, b_out), (c, c_buf, c_out)]
+    for m, (src, buf, _) in enumerate(moves):
+        pltpu.make_async_copy(src, buf, s_in.at[m]).start()
+    for m, (src, buf, dst) in enumerate(moves):
+        pltpu.make_async_copy(src, buf, s_in.at[m]).wait()
+        pltpu.make_async_copy(buf, dst, s_out.at[m]).start()
+    for m, (_, buf, dst) in enumerate(moves):
+        pltpu.make_async_copy(buf, dst, s_out.at[m]).wait()
 
 
 def layer_body(tokens, positions, lengths, norm_attn, norm_mlp, q_gain, k_gain, w_query, w_key, w_value, w_out, w_gate, w_up, w_down, tp_size):
@@ -645,12 +653,12 @@
     parts = 4 * prompts
     block = rows_n // parts
     out, kc, vc = pl.pallas_call(
-        copy_kernel,
+        functools.partial(copy_kernel, rows_n),
         name='copy_out',
-        grid=(parts,),
         out_shape=(jax.ShapeDtypeStruct((rows_n, hidden), BF), jax.ShapeDtypeStruct(kc.shape, BF), jax.ShapeDtypeStruct(vc.shape, BF)),
-        in_specs=[pl.BlockSpec((block, hidden), lambda b: (b + parts, 0))] + [pl.BlockSpec((block, head_dim), lambda b: (b, 0))] * 2,
-        out_specs=[pl.BlockSpec((block, hidden), lambda b: (b, 0))] + [pl.BlockSpec((block, head_dim), lambda b: (b, 0))] * 2,
+        in_specs=[any_spec] * 3,
+        out_specs=[any_spec] * 3,
+        scratch_shapes=[pltpu.VMEM((parts, block, hidden), BF), pltpu.VMEM(kc.shape, BF), pltpu.VMEM(vc.shape, BF), dma((parts + 2,)), dma((parts + 2,))],
         compiler_params=pltpu.CompilerParams(vmem_limit_bytes=60 * 1024 * 1024),
     )(ho, kc, vc)
     return out.reshape(prompts, seq, hidden), kc.reshape(shape), vc.reshape(shape)

time: 480 us -> 473 us (0.985)
  Pallas kernels: 479 us -> 472 us
where the time goes in v2:
time: 473 us
  Pallas kernels  472 us (100%)
    pallas_call x1, Pallas kernels, layer_body(): pl.pallas_call(kernel, name='decoder_layer', out_shape=(jax.ShapeDtypeStr...  455 us
    pallas_call x1, Pallas kernels, layer_body(): pl.pallas_call(functools.partial(copy_kernel, rows_n), name='copy_out', o...  17.2 us

profile of v2, /device:TPU:113, one launch (start us, length us, event | category | flops | bytes accessed | tf_op | source)
XLA Modules:
  0.0 472.8 jit_solution(10070031026087625491)
XLA Ops:
  0.6 454.8 %decoder_layer.1 = (bf16[4608,5120]{1,0:T(8,128)(2,1)}, bf16[2304,128]{1,0:T(8,128)(2,1)}, bf16[2304,128]{1,0:T(8,128)(2,1)}) custom-call(bf16[2304,5120]{1,0:T(8,128)(2,1)} %bitcast.8, s32[3,768]{1,0:T(4,128)} %positions.1, s32[3]{0:T(128)} %lens.1, bf16[5120]{0:T(1024)(128)(2,1)} %n_attn.1, bf16[5120]{0:T(1024)(128)(2,1)} %n_mlp.1, bf16[128]{0:T(256)(128)(2,1)} %q_gain.1, ...), custom_call_target="tpu_custom_call" | custom-call | tf_op jit(solution)/shard_map/decoder_layer/pallas_call | solution.py:621
  455.5 17.2 %copy_out.1 = (bf16[2304,5120]{1,0:T(8,128)(2,1)}, bf16[2304,128]{1,0:T(8,128)(2,1)}, bf16[2304,128]{1,0:T(8,128)(2,1)}) custom-call(bf16[4608,5120]{1,0:T(8,128)(2,1)} %get-tuple-element.9.a, bf16[2304,128]{1,0:T(8,128)(2,1)} %get-tuple-element.10.b, bf16[2304,128]{1,0:T(8,128)(2,1)} %get-tuple-element.11.c), custom_call_target="tpu_custom_call" | custom-call | tf_op jit(solution)/shard_map/copy_out/pallas_call | solution.py:655

commit v3 on v2

--- a/solution.py
+++ b/solution.py
@@ -506,8 +506,8 @@
     start_all(load_rows(ho, 0))
     with jax.named_scope('norm_h'):
         norm_all(1)
-    starts = [(m + 1) * per_ar + v for m, v in zip(range(prompts), (lead, 18, 32))]
-    mids = [(m + 2) * per_ar + v for m, v in zip(range(prompts), (3, 15, 30))]
+    starts = [(m + 1) * per_ar + v for m, v in zip(range(prompts), (lead, 20, 34))]
+    mids = [(m + 2) * per_ar + v for m, v in zip(range(prompts), (3, 17, 30))]
     ones = [max((m + 2) * per_ar + lead, mids[m] + 2) if m + 1 < prompts else mids[m] for m in range(prompts)]
     ends = starts[1:] + [last * per_ar + UNITS * UNITS]
 

time: 473 us -> 473 us (level)
  no operation moved by 1% of the time
where the time goes in v3:
time: 473 us
  Pallas kernels  472 us (100%)
    pallas_call x1, Pallas kernels, layer_body(): pl.pallas_call(kernel, name='decoder_layer', out_shape=(jax.ShapeDtypeStr...  455 us
    pallas_call x1, Pallas kernels, layer_body(): pl.pallas_call(functools.partial(copy_kernel, rows_n), name='copy_out', o...  17.2 us

profile of v3, /device:TPU:113, one launch (start us, length us, event | category | flops | bytes accessed | tf_op | source)
XLA Modules:
  0.0 472.8 jit_solution(16246433640579542257)
XLA Ops:
  0.6 454.8 %decoder_layer.1 = (bf16[4608,5120]{1,0:T(8,128)(2,1)}, bf16[2304,128]{1,0:T(8,128)(2,1)}, bf16[2304,128]{1,0:T(8,128)(2,1)}) custom-call(bf16[2304,5120]{1,0:T(8,128)(2,1)} %bitcast.8, s32[3,768]{1,0:T(4,128)} %positions.1, s32[3]{0:T(128)} %lens.1, bf16[5120]{0:T(1024)(128)(2,1)} %n_attn.1, bf16[5120]{0:T(1024)(128)(2,1)} %n_mlp.1, bf16[128]{0:T(256)(128)(2,1)} %q_gain.1, ...), custom_call_target="tpu_custom_call" | custom-call | tf_op jit(solution)/shard_map/decoder_layer/pallas_call | solution.py:621
  455.5 17.2 %copy_out.1 = (bf16[2304,5120]{1,0:T(8,128)(2,1)}, bf16[2304,128]{1,0:T(8,128)(2,1)}, bf16[2304,128]{1,0:T(8,128)(2,1)}) custom-call(bf16[4608,5120]{1,0:T(8,128)(2,1)} %get-tuple-element.9.a, bf16[2304,128]{1,0:T(8,128)(2,1)} %get-tuple-element.10.b, bf16[2304,128]{1,0:T(8,128)(2,1)} %get-tuple-element.11.c), custom_call_target="tpu_custom_call" | custom-call | tf_op jit(solution)/shard_map/copy_out/pallas_call | solution.py:655
